TPU v7x, 32 devices: a whole 2x2x4 slice. The times are simulated.
32 devices in a mesh: grp: 4 (over y, x), mem: 8 (over z, core).
Axes of the slice: x: 2, y: 2, z: 4, core: 2. Of those that a mesh axis runs over, the one named last changes fastest.
Arguments:
- weight: bfloat16 [2, 16384, 16384], P(None, None, ('grp', 'mem')), may hold values from -0.046875 to 0.046875
- activation: bfloat16 [2, 16384, 512], P(None, ('grp', 'mem')), may hold values from -6 to 6
- points: int32 [4], replicated, may hold values from 0 to 3, each once
Outputs:
- share: float32 [4, 16384, 512], P('grp', 'mem')
Inputs may be any that keep to these rules, and one draw needn't show every extreme that they name: A permutation of 0 to 3; group g evaluates at points[g] + 1.
All inputs are finite; a program needn't handle non-finite values.
Results may differ from a plain program's by a relative error of at most 0.0042.
Values may be sent and summed in bfloat16 or wider, within the bound.
A program may use at most 320 MiB of HBM per device.

v0:
```python
import jax
import jax.numpy as jnp
from jax import lax
from jax.sharding import PartitionSpec as P


def code_stack(raw_blocks, factors):
    total = factors[:, 0, None, None] * raw_blocks[0].astype(jnp.float32)[None]
    for block in range(1, raw_blocks.shape[0]):
        total = total + factors[:, block, None, None] * raw_blocks[block].astype(jnp.float32)[None]
    return total.astype(jnp.bfloat16)


def per_device(weight, activation, points):
    groups = lax.axis_size("grp")
    blocks = weight.shape[0]
    splits = activation.shape[0]
    anchors = (points + 1).astype(jnp.float32) / groups
    factors = anchors[:, None] ** jnp.arange(blocks, dtype=jnp.float32)[None, :]
    lifts_all = anchors[:, None] ** (jnp.arange(splits, dtype=jnp.float32) * blocks)[None, :]
    slab = lax.all_to_all(weight, "mem", split_axis=1, concat_axis=2, tiled=True)
    block_input = lax.all_gather(activation, "mem", axis=1, tiled=True)
    coded_weight = code_stack(slab, factors)
    coded_input = code_stack(block_input, lifts_all)
    return lax.psum_scatter(
        jnp.einsum("grk,gkc->grc", coded_weight, coded_input, preferred_element_type=jnp.float32),
        "grp",
        scatter_dimension=0,
        tiled=True,
    )


def solution(mesh):
    placed = (P(None, None, ("grp", "mem")), P(None, ("grp", "mem"), None), P())
    return jax.shard_map(
        per_device, mesh=mesh, in_specs=placed, out_specs=P("grp", "mem", None), check_vma=False
    )
```

profile of v0, /device:TPU:0, one launch (start us, length us, event | category | flops | bytes accessed | tf_op | source)
XLA Modules:
  0.0 1254.2 jit_solution(2382327408538441488)
XLA Ops:
  6.5 60.1 %copy.10 = bf16[2,16384,512]{2,0,1:T(2,128)(2,1)} copy(bf16[2,16384,512]{2,1,0:T(8,128)(2,1)} %param.3) | data formatting | bytes 67108864 | tf_op args[0]
  66.6 0.0 copy-start
  66.6 7.2 all-to-all-start
  73.9 0.0 all-gather.2.cloned.1.call-start
  73.9 0.7 all-gather.2.cloned.1.call-update
  74.6 0.0 reduce-scatter.4.cloned.1.call-start
  74.7 0.0 copy-done
  74.7 0.1 broadcast_power_fusion
  74.8 154.4 %all-gather.2.cloned.1.call-done = bf16[2,4096,512]{2,1,0:T(8,128)(2,1)} async-done(((bf16[2,512,512]{2,1,0:T(8,128)(2,1)}), bf16[2,4096,512]{2,1,0:T(8,128)(2,1)}) %all-gather.2.cloned.1.call-update) | async-done | bytes 8388624 | tf_op jit(solution)/shard_map/all_gather | solution.py:22
  229.1 11.7 fusion.10
  240.9 15.1 %add_convert_fusion.10 = bf16[4,4096,512]{2,1,0:T(8,128)(2,1)} fusion(f32[4096,512]{1,0:T(8,128)} %get-tuple-element.8, f32[4]{0:T(128)S(1)} %get-tuple-element.10, f32[4096,512]{1,0:T(8,128)} %get-tuple-element.7, f32[4]{0:T(128)S(1)} %get-tuple-element.9), kind=kLoop, calls=%fused_computation.6.clone.clone.2 | loop fusion | flops 33554432 | bytes 33554464 | tf_op jit(solution)/shard_map/grk,gkc->grc/dot_general | solution.py:26
  256.0 609.3 %all-to-all-done = bf16[2,16384,512]{2,0,1:T(2,128)(2,1)} async-done(((bf16[2,16384,512]{2,0,1:T(2,128)(2,1)}), bf16[2,16384,512]{2,0,1:T(2,128)(2,1)}, u32[]{:S(2)}, u32[]{:S(2)}) %all-to-all-start) | async-done | bytes 33554464 | tf_op jit(solution)/shard_map/all_to_all | solution.py:21
  865.3 22.7 %copy.11 = bf16[2,16384,512]{2,1,0:T(8,128)(2,1)} copy(bf16[2,16384,512]{2,0,1:T(2,128)(2,1)} %all-to-all-done) | data formatting | bytes 67108864 | tf_op jit(solution)/shard_map/all_to_all | solution.py:21
  888.0 34.1 %slice_convert_fusion.1 = (f32[1,2048,8,512]{3,1,2,0:T(8,128)}, f32[1,2048,8,512]{3,1,2,0:T(8,128)}) fusion(bf16[2,2048,8,512]{3,1,2,0:T(8,128)(2,1)} %bitcast.25), kind=kLoop, calls=%fused_computation.8 | loop fusion | flops 16777216 | bytes 100663296 | tf_op jit(solution)/shard_map/convert_element_type | solution.py:8
  922.1 31.8 %copy.14 = f32[1,2048,8,512]{1,3,2,0:T(8,128)} copy(f32[1,2048,8,512]{3,1,2,0:T(8,128)} %get-tuple-element.6) | data formatting | bytes 67108864 | tf_op jit(solution)/shard_map/convert_element_type | solution.py:10
  953.9 31.1 %copy.15 = f32[2048,4096]{1,0:T(8,128)} copy(f32[2048,4096]{0,1:T(8,128)} %bitcast.26) | data formatting | bytes 67108864 | tf_op jit(solution)/shard_map/convert_element_type | solution.py:10
  985.0 31.8 %copy.12 = f32[1,2048,8,512]{1,3,2,0:T(8,128)} copy(f32[1,2048,8,512]{3,1,2,0:T(8,128)} %get-tuple-element.5) | data formatting | bytes 67108864 | tf_op jit(solution)/shard_map/convert_element_type | solution.py:8
  1016.8 31.1 %copy.13 = f32[2048,4096]{1,0:T(8,128)} copy(f32[2048,4096]{0,1:T(8,128)} %bitcast.27) | data formatting | bytes 67108864 | tf_op jit(solution)/shard_map/convert_element_type | solution.py:8
  1047.9 46.0 %fusion = f32[4,2048,512]{2,1,0:T(8,128)} fusion(f32[2048,4096]{1,0:T(8,128)} %copy.15, f32[4]{0:T(128)S(1)} %get-tuple-element.15, f32[2048,4096]{1,0:T(8,128)} %copy.13, f32[4]{0:T(128)S(1)} %get-tuple-element.16, bf16[4,4096,512]{2,1,0:T(8,128)(2,1)} %add_convert_fusion.10), kind=kOutput, calls=%fused_computation.1 | convolution fusion | flops 34493956096 | bytes 100663328 | tf_op jit(solution)/shard_map/grk,gkc->grc/dot_general | solution.py:26
  1093.9 0.0 reduce-scatter.4.cloned.1.call-update
  1094.0 153.4 %reduce-scatter.4.cloned.1.call-done = f32[1,2048,512]{2,1,0:T(8,128)} async-done(((f32[4,2048,512]{2,1,0:T(8,128)}), f32[1,2048,512]{2,1,0:T(8,128)}) %reduce-scatter.4.cloned.1.call-update) | async-done | bytes 4194320
  (3 shorter events, 0.0 us)
Async XLA Ops:
  66.6 8.0 copy-start
  66.6 798.7 %all-to-all-start = ((bf16[2,16384,512]{2,0,1:T(2,128)(2,1)}), bf16[2,16384,512]{2,0,1:T(2,128)(2,1)}, u32[]{:S(2)}, u32[]{:S(2)}) async-start(bf16[2,16384,512]{2,0,1:T(2,128)(2,1)} %copy.10), calls=%async_computation | async-start | bytes 67108864 | tf_op jit(solution)/shard_map/all_to_all | solution.py:21
  73.9 155.3 %all-gather.2.cloned.1.call-start = ((), (), s32[]{:S(2)}) async-start(), calls=%async_computation.2 | async-start | bytes 9437184 | tf_op jit(solution)/shard_map/all_gather | solution.py:22
  74.6 1172.8 %reduce-scatter.4.cloned.1.call-start = ((), (), s32[]{:S(2)}) async-start(), calls=%async_computation.3 | async-start | bytes 20971520
Sparse Core Ops, SparseCore 0:
  76.3 152.8 all-gather.1
  1094.1 153.2 reduce-scatter.3
where the time goes:
time: 1260 us; the launch traced here: 1250 us
  waiting for transfers between devices  918 us (73%)
  local copies, waits for them, and re-layouts  209 us (17%)
  other arithmetic  60.9 us (5%)
  matrix products  46 us (4%)
  between operations  13.5 us (1%)
    all_to_all x1, waiting for transfers between devices, per_device(): lax.all_to_all(weight, 'mem', split_axis=1, concat_axis=2, tiled=True)  609 us
    all_gather x1, waiting for transfers between devices, per_device(): block_input = lax.all_gather(activation, 'mem', axis=1, tiled=True)  154 us
    unnamed x3, waiting for transfers between devices  154 us
    convert_element_type x2, local copies, waits for them, and re-layouts, code_stack(): raw_blocks[block].astype(jnp.float32)[None]  62.9 us
    convert_element_type x2, local copies, waits for them, and re-layouts, code_stack(): total = factors[:, 0, None, None] * raw_blocks[0].astype(jnp.float32)[None]  62.9 us
    unnamed x3, local copies, waits for them, and re-layouts  60.1 us
    dot_general x1, matrix products, per_device(): jnp.einsum('grk,gkc->grc', coded_weight, coded_input, preferred_element_t...  46 us
    convert_element_type x1, other arithmetic, code_stack(): total = factors[:, 0, None, None] * raw_blocks[0].astype(jnp.float32)[None]  34.1 us
  transfers between devices with their start and end apart: 3, of which 3 were waited for; matrix products, arithmetic and copies ran while one was open for 2% of the time, Pallas kernels for 0%

commit v1 on v0

--- a/solution.py
+++ b/solution.py
@@ -19,7 +19,9 @@
     factors = anchors[:, None] ** jnp.arange(blocks, dtype=jnp.float32)[None, :]
     lifts_all = anchors[:, None] ** (jnp.arange(splits, dtype=jnp.float32) * blocks)[None, :]
     slab = lax.all_to_all(weight, "mem", split_axis=1, concat_axis=2, tiled=True)
-    block_input = lax.all_gather(activation, "mem", axis=1, tiled=True)
+    block_input = jnp.concatenate(
+        lax.all_to_all(jnp.stack([activation] * lax.axis_size("mem")), "mem", 0, 0), axis=1
+    )
     coded_weight = code_stack(slab, factors)
     coded_input = code_stack(block_input, lifts_all)
     return lax.psum_scatter(

time: 1260 us -> 1320 us (1.048)
  waiting for transfers between devices: 918 us -> 969 us
    all_gather x1 -> x0, waiting for transfers between devices: 154 us -> none  [per_device(): block_input = lax.all_gather(activation, 'mem', axis=1, tiled=True)]
    all_to_all x0 -> x1, waiting for transfers between devices: none -> 124 us  [per_device(): lax.all_to_all(jnp.stack([activation] * lax.axis_size('mem')), 'mem', 0, 0)]
    all_to_all x1, waiting for transfers between devices: 609 us -> 692 us  [per_device(): lax.all_to_all(weight, 'mem', split_axis=1, concat_axis=2, tiled=True)]
    unnamed x3 -> x2, waiting for transfers between devices: 154 us -> 153 us
  transfers between devices with their start and end apart: 3 -> 3, of which waited for: 3 -> 3; matrix products, arithmetic and copies ran while one was open for 2% -> 7% of each run, Pallas kernels for 0% -> 0%
where the time goes in v1:
time: 1320 us
  waiting for transfers between devices  969 us (73%)
  local copies, waits for them, and re-layouts  219 us (17%)
  other arithmetic  59.6 us (5%)
  matrix products  46 us (3%)
  starting transfers between devices  13.7 us (1%)
  between operations  13.4 us (1%)
    all_to_all x1, waiting for transfers between devices, per_device(): lax.all_to_all(weight, 'mem', split_axis=1, concat_axis=2, tiled=True)  692 us
    unnamed x2, waiting for transfers between devices  153 us
    all_to_all x1, waiting for transfers between devices, per_device(): lax.all_to_all(jnp.stack([activation] * lax.axis_size('mem')), 'mem', 0, 0)  124 us
    convert_element_type x2, local copies, waits for them, and re-layouts, code_stack(): raw_blocks[block].astype(jnp.float32)[None]  62.9 us
    convert_element_type x2, local copies, waits for them, and re-layouts, code_stack(): total = factors[:, 0, None, None] * raw_blocks[0].astype(jnp.float32)[None]  62.9 us
    unnamed x3, local copies, waits for them, and re-layouts  60.1 us
    dot_general x1, matrix products, per_device(): jnp.einsum('grk,gkc->grc', coded_weight, coded_input, preferred_element_t...  46 us
    convert_element_type x1, other arithmetic, code_stack(): total = factors[:, 0, None, None] * raw_blocks[0].astype(jnp.float32)[None]  34.1 us
  transfers between devices with their start and end apart: 3, of which 3 were waited for; matrix products, arithmetic and copies ran while one was open for 7% of the time, Pallas kernels for 0%

profile of v1, /device:TPU:0, one launch (start us, length us, event | category | flops | bytes accessed | tf_op | source)
XLA Modules:
  0.0 1320.7 jit_solution(5928210221372490084)
XLA Ops:
  6.5 5.3 stack.2
  11.8 6.4 all-to-all-start.1
  18.1 60.1 %copy.10 = bf16[2,16384,512]{2,0,1:T(2,128)(2,1)} copy(bf16[2,16384,512]{2,1,0:T(8,128)(2,1)} %param.3) | data formatting | bytes 67108864 | tf_op args[0]
  78.2 0.0 copy-start
  78.3 123.9 %all-to-all-done.1 = bf16[8,2,512,512]{3,2,1,0:T(8,128)(2,1)} async-done(((bf16[8,2,512,512]{3,2,1,0:T(8,128)(2,1)}), bf16[8,2,512,512]{3,2,1,0:T(8,128)(2,1)}, u32[]{:S(2)}, u32[]{:S(2)}) %all-to-all-start.1) | async-done | bytes 8388640 | tf_op jit(solution)/shard_map/all_to_all | solution.py:23
  202.1 7.1 all-to-all-start
  209.2 0.2 reduce-scatter.4.cloned.1.call-start
  209.4 0.0 copy-done
  209.5 0.1 broadcast_power_fusion
  209.6 5.3 fusion.9
  214.8 10.4 bitcast_convert_fusion
  225.3 15.1 %add_convert_fusion.10 = bf16[4,4096,512]{2,1,0:T(8,128)(2,1)} fusion(f32[4096,512]{1,0:T(8,128)} %get-tuple-element.17, f32[4]{0:T(128)S(1)} %get-tuple-element.10, f32[4096,512]{1,0:T(8,128)} %get-tuple-element.18, f32[4]{0:T(128)S(1)} %get-tuple-element.9), kind=kLoop, calls=%fused_computation.6.clone.clone.2 | loop fusion | flops 33554432 | bytes 33554464 | tf_op jit(solution)/shard_map/grk,gkc->grc/dot_general | solution.py:28
  240.4 692.0 %all-to-all-done = bf16[2,16384,512]{2,0,1:T(2,128)(2,1)} async-done(((bf16[2,16384,512]{2,0,1:T(2,128)(2,1)}), bf16[2,16384,512]{2,0,1:T(2,128)(2,1)}, u32[]{:S(2)}, u32[]{:S(2)}) %all-to-all-start) | async-done | bytes 33554464 | tf_op jit(solution)/shard_map/all_to_all | solution.py:21
  932.4 22.7 %copy.11 = bf16[2,16384,512]{2,1,0:T(8,128)(2,1)} copy(bf16[2,16384,512]{2,0,1:T(2,128)(2,1)} %all-to-all-done) | data formatting | bytes 67108864 | tf_op jit(solution)/shard_map/all_to_all | solution.py:21
  955.1 34.1 %slice_convert_fusion.1 = (f32[1,2048,8,512]{3,1,2,0:T(8,128)}, f32[1,2048,8,512]{3,1,2,0:T(8,128)}) fusion(bf16[2,2048,8,512]{3,1,2,0:T(8,128)(2,1)} %bitcast.22), kind=kLoop, calls=%fused_computation.8 | loop fusion | flops 16777216 | bytes 100663296 | tf_op jit(solution)/shard_map/convert_element_type | solution.py:8
  989.1 31.8 %copy.14 = f32[1,2048,8,512]{1,3,2,0:T(8,128)} copy(f32[1,2048,8,512]{3,1,2,0:T(8,128)} %get-tuple-element.6) | data formatting | bytes 67108864 | tf_op jit(solution)/shard_map/convert_element_type | solution.py:10
  1020.9 31.1 %copy.15 = f32[2048,4096]{1,0:T(8,128)} copy(f32[2048,4096]{0,1:T(8,128)} %bitcast.23) | data formatting | bytes 67108864 | tf_op jit(solution)/shard_map/convert_element_type | solution.py:10
  1052.0 31.8 %copy.12 = f32[1,2048,8,512]{1,3,2,0:T(8,128)} copy(f32[1,2048,8,512]{3,1,2,0:T(8,128)} %get-tuple-element.5) | data formatting | bytes 67108864 | tf_op jit(solution)/shard_map/convert_element_type | solution.py:8
  1083.8 31.1 %copy.13 = f32[2048,4096]{1,0:T(8,128)} copy(f32[2048,4096]{0,1:T(8,128)} %bitcast.24) | data formatting | bytes 67108864 | tf_op jit(solution)/shard_map/convert_element_type | solution.py:8
  1114.9 46.0 %fusion = f32[4,2048,512]{2,1,0:T(8,128)} fusion(f32[2048,4096]{1,0:T(8,128)} %copy.15, f32[4]{0:T(128)S(1)} %get-tuple-element.15, f32[2048,4096]{1,0:T(8,128)} %copy.13, f32[4]{0:T(128)S(1)} %get-tuple-element.16, bf16[4,4096,512]{2,1,0:T(8,128)(2,1)} %add_convert_fusion.10), kind=kOutput, calls=%fused_computation.1 | convolution fusion | flops 34493956096 | bytes 100663328 | tf_op jit(solution)/shard_map/grk,gkc->grc/dot_general | solution.py:28
  1161.0 0.0 reduce-scatter.4.cloned.1.call-update
  1161.0 152.8 %reduce-scatter.4.cloned.1.call-done = f32[1,2048,512]{2,1,0:T(8,128)} async-done(((f32[4,2048,512]{2,1,0:T(8,128)}), f32[1,2048,512]{2,1,0:T(8,128)}) %reduce-scatter.4.cloned.1.call-update) | async-done | bytes 4194320
  (3 shorter events, 0.0 us)
Async XLA Ops:
  11.8 190.3 %all-to-all-start.1 = ((bf16[8,2,512,512]{3,2,1,0:T(8,128)(2,1)}), bf16[8,2,512,512]{3,2,1,0:T(8,128)(2,1)}, u32[]{:S(2)}, u32[]{:S(2)}) async-start(bf16[8,2,512,512]{3,2,1,0:T(8,128)(2,1)} %stack.2), calls=%async_computation.1 | async-start | bytes 16777216 | tf_op jit(solution)/shard_map/all_to_all | solution.py:23
  78.2 131.2 %copy-start = (s32[4]{0:T(128)S(1)}, s32[4]{0:T(128)}, u32[]{:S(2)}) copy-start(s32[4]{0:T(128)} %param.5) | copy-start | bytes 52
  202.1 730.3 %all-to-all-start = ((bf16[2,16384,512]{2,0,1:T(2,128)(2,1)}), bf16[2,16384,512]{2,0,1:T(2,128)(2,1)}, u32[]{:S(2)}, u32[]{:S(2)}) async-start(bf16[2,16384,512]{2,0,1:T(2,128)(2,1)} %copy.10), calls=%async_computation | async-start | bytes 67108864 | tf_op jit(solution)/shard_map/all_to_all | solution.py:21
  209.2 1104.6 %reduce-scatter.4.cloned.1.call-start = ((), (), s32[]{:S(2)}) async-start(), calls=%async_computation.3 | async-start | bytes 20971520
Sparse Core Ops, SparseCore 0:
  1161.1 152.6 reduce-scatter.3

commit v2 on v0

--- a/solution.py
+++ b/solution.py
@@ -18,7 +18,10 @@
     anchors = (points + 1).astype(jnp.float32) / groups
     factors = anchors[:, None] ** jnp.arange(blocks, dtype=jnp.float32)[None, :]
     lifts_all = anchors[:, None] ** (jnp.arange(splits, dtype=jnp.float32) * blocks)[None, :]
-    slab = lax.all_to_all(weight, "mem", split_axis=1, concat_axis=2, tiled=True)
+    slab = jnp.concatenate(
+        lax.all_to_all(jnp.stack(jnp.split(weight, lax.axis_size("mem"), axis=1)), "mem", 0, 0),
+        axis=2,
+    )
     block_input = lax.all_gather(activation, "mem", axis=1, tiled=True)
     coded_weight = code_stack(slab, factors)
     coded_input = code_stack(block_input, lifts_all)

time: 1260 us -> 1260 us (level)
    convert_element_type x2 -> x1, local copies, waits for them, and re-layouts: 62.9 us -> 31.1 us  [code_stack(): total = factors[:, 0, None, None] * raw_blocks[0].astype(jnp.float32)[None]]
    convert_element_type x2 -> x1, local copies, waits for them, and re-layouts: 62.9 us -> 31.2 us  [code_stack(): raw_blocks[block].astype(jnp.float32)[None]]
    split x0 -> x1, local copies, waits for them, and re-layouts: none -> 23.7 us  [per_device(): jnp.split(weight, lax.axis_size('mem'), axis=1)]
    slice x0 -> x1, local copies, waits for them, and re-layouts: none -> 23.5 us  [code_stack(): total = factors[:, 0, None, None] * raw_blocks[0].astype(jnp.float32)[None]]
    unnamed x3 -> x27, local copies, waits for them, and re-layouts: 60.1 us -> 75.1 us
where the time goes in v2:
time: 1260 us
  waiting for transfers between devices  918 us (73%)
  local copies, waits for them, and re-layouts  210 us (17%)
  other arithmetic  60.7 us (5%)
  matrix products  46 us (4%)
  between operations  13.5 us (1%)
    all_to_all x1, waiting for transfers between devices, per_device(): lax.all_to_all(jnp.stack(jnp.split(weight, lax.axis_size('mem'), axis=1))...  609 us
    all_gather x1, waiting for transfers between devices, per_device(): block_input = lax.all_gather(activation, 'mem', axis=1, tiled=True)  154 us
    unnamed x3, waiting for transfers between devices  154 us
    unnamed x27, local copies, waits for them, and re-layouts  75.1 us
    dot_general x1, matrix products, per_device(): jnp.einsum('grk,gkc->grc', coded_weight, coded_input, preferred_element_t...  46 us
    convert_element_type x1, other arithmetic, code_stack(): raw_blocks[block].astype(jnp.float32)[None]  33.8 us
    convert_element_type x1, local copies, waits for them, and re-layouts, code_stack(): raw_blocks[block].astype(jnp.float32)[None]  31.2 us
    convert_element_type x1, local copies, waits for them, and re-layouts, code_stack(): total = factors[:, 0, None, None] * raw_blocks[0].astype(jnp.float32)[None]  31.1 us
  transfers between devices with their start and end apart: 3, of which 3 were waited for; matrix products, arithmetic and copies ran while one was open for 2% of the time, Pallas kernels for 0%

profile of v2, /device:TPU:0, one launch (start us, length us, event | category | flops | bytes accessed | tf_op | source)
XLA Modules:
  0.0 1255.1 jit_solution(18180500791674269142)
XLA Ops:
  6.5 23.7 %fusion.12 = (bf16[2,2048,512]{2,1,0:T(8,128)(2,1)}, bf16[2,2048,512]{2,1,0:T(8,128)(2,1)}, bf16[2,2048,512]{2,1,0:T(8,128)(2,1)}, bf16[2,2048,512]{2,1,0:T(8,12...) fusion(bf16[2,16384,512]{2,1,0:T(8,128)(2,1)} %param.3), kind=kLoop, calls=%fused_computation.35 | loop fusion | bytes 67108864 | tf_op jit(solution)/shard_map/split | solution.py:22
  30.3 6.3 copy.25
  36.6 4.7 bitcast_dynamic-update-slice_fusion.7
  41.4 6.3 copy.26
  47.6 6.3 copy.27
  54.0 6.3 copy.28
  60.3 6.4 copy.29
  66.6 6.3 copy.30
  72.9 6.3 copy.31
  79.2 6.3 copy.32
  85.5 0.0 copy-start.4
  85.5 0.0 copy-start.3
  85.5 0.0 copy-start.2
  85.5 5.1 bitcast_dynamic-update-slice_fusion.6
  90.5 0.0 copy-start
  90.5 5.5 bitcast_dynamic-update-slice_fusion.5
  96.1 0.0 copy-done.4
  96.1 0.0 copy-start.1
  96.1 2.4 bitcast_dynamic-update-slice_fusion.4
  98.5 0.0 copy-done.3
  98.5 2.3 bitcast_dynamic-update-slice_fusion.3
  100.8 0.0 copy-done.2
  100.8 2.3 bitcast_dynamic-update-slice_fusion.2
  103.1 0.0 copy-done
  103.1 2.3 bitcast_dynamic-update-slice_fusion.1
  105.4 0.0 copy-done.1
  105.4 2.2 bitcast_dynamic-update-slice_fusion
  107.6 0.0 copy-start.5
  107.6 7.3 all-to-all-start
  115.0 0.0 all-gather.2.cloned.1.call-start
  115.0 0.7 all-gather.2.cloned.1.call-update
  115.7 0.2 reduce-scatter.4.cloned.1.call-start
  115.9 0.0 copy-done.5
  116.0 0.1 broadcast_power_fusion
  116.1 154.3 %all-gather.2.cloned.1.call-done = bf16[2,4096,512]{2,1,0:T(8,128)(2,1)} async-done(((bf16[2,512,512]{2,1,0:T(8,128)(2,1)}), bf16[2,4096,512]{2,1,0:T(8,128)(2,1)}) %all-gather.2.cloned.1.call-update) | async-done | bytes 8388624 | tf_op jit(solution)/shard_map/all_gather | solution.py:25
  270.3 11.7 fusion.10
  282.0 15.1 %add_convert_fusion.10 = bf16[4,4096,512]{2,1,0:T(8,128)(2,1)} fusion(f32[4096,512]{1,0:T(8,128)} %get-tuple-element.16, f32[4]{0:T(128)S(1)} %get-tuple-element.18, f32[4096,512]{1,0:T(8,128)} %get-tuple-element.15, f32[4]{0:T(128)S(1)} %get-tuple-element.17), kind=kLoop, calls=%fused_computation.7.clone.clone.2 | loop fusion | flops 33554432 | bytes 33554464 | tf_op jit(solution)/shard_map/grk,gkc->grc/dot_general | solution.py:29
  297.2 609.1 %all-to-all-done = bf16[8,2,2048,512]{2,3,1,0:T(8,128)(2,1)} async-done(((bf16[8,2,2048,512]{2,3,1,0:T(8,128)(2,1)}), bf16[8,2,2048,512]{2,3,1,0:T(8,128)(2,1)}, u32[]{:S(2)}, u32[]{:S(2)}) %all-to-all-start) | async-done | bytes 33554464 | tf_op jit(solution)/shard_map/all_to_all | solution.py:22
  906.3 22.8 %copy.34 = bf16[8,2,2048,512]{2,3,0,1:T(8,128)(2,1)} copy(bf16[8,2,2048,512]{2,3,1,0:T(8,128)(2,1)} %all-to-all-done) | data formatting | bytes 67108864 | tf_op jit(solution)/shard_map/all_to_all | solution.py:22
  929.1 23.5 %fusion.11 = (bf16[1,2048,8,512]{1,3,2,0:T(8,128)(2,1)}, bf16[1,2048,8,512]{1,3,2,0:T(8,128)(2,1)}) fusion(bf16[2,2048,8,512]{1,3,2,0:T(8,128)(2,1)} %bitcast.45), kind=kLoop, calls=%fused_computation.34 | loop fusion | bytes 67108864 | tf_op jit(solution)/shard_map/slice | solution.py:8
  952.6 33.8 %bitcast_convert_fusion = (f32[2048,4096]{0,1:T(8,128)}, f32[2048,4096]{0,1:T(8,128)}) fusion(bf16[1,2048,8,512]{1,3,2,0:T(8,128)(2,1)} %get-tuple-element.6, bf16[1,2048,8,512]{1,3,2,0:T(8,128)(2,1)} %get-tuple-element.5), kind=kLoop, calls=%fused_computation.8 | loop fusion | flops 16777216 | bytes 100663296 | tf_op jit(solution)/shard_map/convert_element_type | solution.py:10
  986.4 31.1 %copy.23 = f32[2048,4096]{1,0:T(8,128)} copy(f32[2048,4096]{0,1:T(8,128)} %get-tuple-element.24) | data formatting | bytes 67108864 | tf_op jit(solution)/shard_map/convert_element_type | solution.py:8
  1017.5 31.2 %copy.24 = f32[2048,4096]{1,0:T(8,128)} copy(f32[2048,4096]{0,1:T(8,128)} %get-tuple-element.23) | data formatting | bytes 67108864 | tf_op jit(solution)/shard_map/convert_element_type | solution.py:10
  1048.7 46.0 %fusion = f32[4,2048,512]{2,1,0:T(8,128)} fusion(f32[2048,4096]{1,0:T(8,128)} %copy.24, f32[4]{0:T(128)S(1)} %get-tuple-element.25, f32[2048,4096]{1,0:T(8,128)} %copy.23, f32[4]{0:T(128)S(1)} %get-tuple-element.26, bf16[4,4096,512]{2,1,0:T(8,128)(2,1)} %add_convert_fusion.10), kind=kOutput, calls=%fused_computation.1 | convolution fusion | flops 34493956096 | bytes 100663328 | tf_op jit(solution)/shard_map/grk,gkc->grc/dot_general | solution.py:29
  1094.7 0.0 reduce-scatter.4.cloned.1.call-update
  1094.8 153.5 %reduce-scatter.4.cloned.1.call-done = f32[1,2048,512]{2,1,0:T(8,128)} async-done(((f32[4,2048,512]{2,1,0:T(8,128)}), f32[1,2048,512]{2,1,0:T(8,128)}) %reduce-scatter.4.cloned.1.call-update) | async-done | bytes 4194320
  (3 shorter events, 0.0 us)
Async XLA Ops:
  85.5 10.6 copy-start.4
  85.5 13.1 %copy-start.3 = (bf16[2,2048,512]{1,2,0:T(8,128)(2,1)S(1)}, bf16[2,2048,512]{1,2,0:T(8,128)(2,1)}, u32[]{:S(2)}) copy-start(bf16[2,2048,512]{1,2,0:T(8,128)(2,1)} %copy.29) | copy-start | bytes 12582916
  85.5 15.3 %copy-start.2 = (bf16[2,2048,512]{1,2,0:T(8,128)(2,1)S(1)}, bf16[2,2048,512]{1,2,0:T(8,128)(2,1)}, u32[]{:S(2)}) copy-start(bf16[2,2048,512]{1,2,0:T(8,128)(2,1)} %copy.30) | copy-start | bytes 12582916
  90.5 12.6 %copy-start = (bf16[2,2048,512]{1,2,0:T(8,128)(2,1)S(1)}, bf16[2,2048,512]{1,2,0:T(8,128)(2,1)}, u32[]{:S(2)}) copy-start(bf16[2,2048,512]{1,2,0:T(8,128)(2,1)} %copy.31) | copy-start | bytes 12582916
  96.1 9.3 copy-start.1
  107.6 8.3 copy-start.5
  107.6 798.7 %all-to-all-start = ((bf16[8,2,2048,512]{2,3,1,0:T(8,128)(2,1)}), bf16[8,2,2048,512]{2,3,1,0:T(8,128)(2,1)}, u32[]{:S(2)}, u32[]{:S(2)}) async-start(bf16[8,2,2048,512]{2,3,1,0:T(8,128)(2,1)} %bitcast_dynamic-update-slice_fusion), calls=%async_computation | async-start | bytes 67108864 | tf_op jit(solution)/shard_map/all_to_all | solution.py:22
  115.0 155.4 %all-gather.2.cloned.1.call-start = ((), (), s32[]{:S(2)}) async-start(), calls=%async_computation.2 | async-start | bytes 9437184 | tf_op jit(solution)/shard_map/all_gather | solution.py:25
  115.7 1132.6 %reduce-scatter.4.cloned.1.call-start = ((), (), s32[]{:S(2)}) async-start(), calls=%async_computation.3 | async-start | bytes 20971520
Sparse Core Ops, SparseCore 0:
  117.4 152.9 all-gather.1
  1094.9 153.3 reduce-scatter.3
